TPU v7x, 32 devices: a whole 2x2x4 slice. The times are simulated.
32 devices in a mesh: grp: 4 (over y, x), slab: 8 (over z, core).
Axes of the slice: x: 2, y: 2, z: 4, core: 2. Of those that a mesh axis runs over, the one named last changes fastest.
Arguments:
- velocity: float32 [16, 3, 4, 16384], P(None, None, 'grp', 'slab'), may hold values from -6 to 6
- old_basis: bfloat16 [64, 3, 4, 16384], P(None, None, None, 'slab'), may hold values from -6 to 6
- singular_values: float32 [64], replicated, may hold values from 0.7 to 1.4
- thickness: int32 [4, 8], P('grp', 'slab'), may hold values from 1 to 4, as said below
Outputs:
- gram_matrix: float32 [80, 80], replicated
- new_basis: bfloat16 [64, 3, 4, 16384], P(None, None, None, 'slab')
- offsets: int32 [4, 8], P('grp', 'slab')
Inputs may be any that keep to these rules, and one draw needn't show every extreme that they name: `thickness`: the entry at row-major position p differs from 1 + (p * 3) // 32 by at most one. The first entry is 1 and the last is 4.
All inputs are finite; a program needn't handle non-finite values.
Results may differ from a plain program's by a relative error of at most 0.0004.
The roundings to bfloat16 on the way count: a program that leaves them out, or rounds other values in their place, can miss the bound.
Values may be sent and summed in bfloat16 or wider, within the bound.
A program may use at most 64 MiB of HBM per device.

v0:
```python
import jax
import jax.numpy as jnp
from jax import lax
from jax.sharding import PartitionSpec as P

PLANE = 512


def entering(value, axis, join, neutral):
    count, mine = (lax.axis_size(axis), lax.axis_index(axis))
    pieces = lax.all_gather(value, axis)
    total = jnp.full_like(value, 0) + jnp.asarray(neutral, value.dtype)

    def step(position, total):
        longer = join(total, pieces[position])
        return jnp.where(position < mine, longer, total)

    return lax.fori_loop(0, count - 1, step, total)


def orthonormalize(matrix, rank_count):
    iterate = matrix * (0.5 * rank_count**0.5 / jnp.sqrt(jnp.sum(matrix * matrix)))
    for sweep_index in range(4):
        product = jnp.dot(iterate.T, iterate, precision=lax.Precision.HIGHEST)
        iterate = 1.5 * iterate - 0.5 * jnp.dot(iterate, product, precision=lax.Precision.HIGHEST)
    return iterate


def add_counts(earlier, later):
    return earlier + later


def per_device(velocity, old_basis, singular_values, thickness):
    capacity = velocity.shape[-1]
    snap_count = velocity.shape[0]
    rank_count = old_basis.shape[0]
    plane_ids = lax.broadcasted_iota(jnp.int32, (1, capacity), 1) // PLANE
    own_mask = plane_ids < thickness
    masked = jnp.where(
        own_mask[None, None], velocity.astype(jnp.bfloat16), jnp.zeros((), jnp.bfloat16)
    )
    live_cells = lax.psum(jnp.sum(thickness).astype(jnp.float32) * PLANE, ("grp", "slab"))
    region_index = lax.axis_index("grp")
    own_basis = lax.dynamic_slice_in_dim(old_basis, region_index, 1, 2)
    columns = jnp.where(own_mask[None, None], own_basis, jnp.zeros((), jnp.bfloat16))
    stacked = jnp.concatenate([columns.reshape(rank_count, -1), masked.reshape(snap_count, -1)], 0)
    raw_gram = lax.dot_general(
        stacked, stacked, (((1,), (1,)), ((), ())), preferred_element_type=jnp.float32
    )
    partial_terms = (raw_gram,)
    summed = lax.psum((partial_terms[0],), ("grp", "slab"))
    scales = jnp.concatenate([singular_values, jnp.ones((snap_count,), jnp.float32)])
    gram_matrix = summed[0] * scales[:, None] * scales[None, :] / (3.0 * live_cells)
    mixing = orthonormalize(gram_matrix[:, :rank_count], rank_count)
    mixing_rows = (mixing * scales[:, None]).T.astype(jnp.bfloat16)
    updated = jnp.dot(mixing_rows, stacked, preferred_element_type=jnp.float32).astype(jnp.bfloat16)
    new_basis = lax.all_gather(
        updated.reshape(rank_count, 3, 1, capacity), "grp", axis=2, tiled=True
    )
    offsets = entering(thickness, ("grp", "slab"), add_counts, jnp.zeros_like(thickness))
    return (gram_matrix, new_basis, offsets)


def solution(mesh):
    in_specs = (P(None, None, "grp", "slab"), P(None, None, None, "slab"), P(), P("grp", "slab"))
    out_specs = (P(), P(None, None, None, "slab"), P("grp", "slab"))
    return jax.shard_map(
        per_device, mesh=mesh, in_specs=in_specs, out_specs=out_specs, check_vma=False
    )
```

profile of v0, /device:TPU:0, one launch (start us, length us, event | category | flops | bytes accessed | tf_op | source)
XLA Modules:
  0.0 160.7 jit_solution(7786227598539404116)
XLA Ops:
  7.9 2.2 %fusion.7 = bf16[16,3,2048]{2,1,0:T(4,128)(2,1)S(1)} fusion(pred[2048]{0:T(1024)(128)(4,1)S(1)} %fusion.11, f32[16,3,1,2048]{3,2,1,0:T(1,128)} %param.6), kind=kLoop, calls=%fused_computation.15 | loop fusion | flops 196608 | bytes 591872 | tf_op jit(solution)/shard_map/jit(_where)/select_n | solution.py:39
  10.3 7.4 %fusion = bf16[64,3,2048]{2,1,0:T(4,128)(2,1)S(1)} fusion(pred[2048]{0:T(1024)(128)(4,1)S(1)} %fusion.11, bf16[64,3,4,2048]{3,2,1,0:T(4,128)(2,1)} %param.7, s32[]{:T(128)S(6)} %select_n.42), kind=kLoop, calls=%fused_computation.3 | loop fusion | flops 393216 | bytes 1574916 | tf_op jit(solution)/shard_map/jit(_where)/select_n | solution.py:45
  17.7 0.6 copy.29
  19.0 42.7 %all-reduce.2 = (f32[80,80]{1,0:T(8,128)S(1)}, f32[]{:T(128)}) all-reduce(f32[80,80]{1,0:T(8,128)S(1)} %fusion.15, f32[]{:T(128)S(6)} %mul.67), channel_id=1, replica_groups=mesh['grp'=4,'slab'=8] {'grp','slab'}, use_global_device_ids=true, to_apply=%region_0.1 | all-reduce | flops 6401 | bytes 51208 | tf_op jit(solution)/shard_map/psum | solution.py:51
  62.4 0.6 multiply_reduce_fusion
  65.8 1.2 reshape.69
  67.0 1.5 copy.21
  68.5 41.1 %all-reduce.1 = s32[32]{0:T(128)S(1)} all-reduce(s32[32]{0:T(128)S(1)} %bitcast_dynamic-update-slice_fusion), channel_id=2, replica_groups=mesh['grp'=4,'slab'=8] {'grp','slab'}, use_global_device_ids=true, to_apply=%add.1 | all-reduce | flops 32 | bytes 256
  109.7 37.0 %while.13 = (s32[]{:T(128)}, s32[1,1]{1,0:T(1,128)}, s32[]{:T(128)}, s32[32,1,1]{0,2,1:T(1,128)S(1)}, s32[]{:T(128)}) while((s32[]{:T(128)}, s32[1,1]{1,0:T(1,128)}, s32[]{:T(128)}, s32[32,1,1]{0,2,1:T(1,128)S(1)}, s32[]{:T(128)}) %tuple.42), condition=%wide.region_4.5_spmd, body=%wide.region_3.4_spmd.sunk | while | flops 5 | bytes 115 | solution.py:18
  110.8 0.6 constant_dynamic-slice_fusion.2
  112.0 0.6 constant_dynamic-slice_fusion.2
  113.2 0.6 constant_dynamic-slice_fusion.2
  114.4 0.6 constant_dynamic-slice_fusion.2
  118.0 0.6 constant_dynamic-slice_fusion.2
  119.2 0.6 constant_dynamic-slice_fusion.2
  120.4 0.6 constant_dynamic-slice_fusion.2
  121.6 0.6 constant_dynamic-slice_fusion.2
  125.2 0.6 constant_dynamic-slice_fusion.2
  126.4 0.6 constant_dynamic-slice_fusion.2
  127.6 0.6 constant_dynamic-slice_fusion.2
  128.8 0.6 constant_dynamic-slice_fusion.2
  130.0 0.6 constant_dynamic-slice_fusion.2
  133.6 0.6 constant_dynamic-slice_fusion.2
  146.7 6.0 %copy.23 = bf16[64,3,4,2048]{3,2,1,0:T(4,128)(2,1)} copy(bf16[64,3,4,2048]{3,0,1,2:T(8,128)(2,1)} %all-gather.3.cloned.1.call-done) | data formatting | bytes 6291456
  (42 shorter events, 13.1 us)
Async XLA Ops:
  7.2 139.5 %all-gather.3.cloned.1.call-start = ((), (), s32[]{:S(2)}) async-start(), calls=%async_computation | async-start | bytes 3932160 | tf_op jit(solution)/shard_map/all_gather | solution.py:57
  18.3 0.7 copy-start.1
  62.4 4.6 %copy-start = (f32[80,80]{1,0:T(8,128)}, f32[80,80]{1,0:T(8,128)S(1)}, u32[]{:S(2)}) copy-start(f32[80,80]{1,0:T(8,128)S(1)} %multiply_divide_fusion) | copy-start | bytes 76804
Sparse Core Ops, SparseCore 0:
  68.6 44.5 all-gather.2
where the time goes:
time: 161 us
  blocking collectives  83.8 us (52%)
  local copies, waits for them, and re-layouts  27.9 us (17%)
  loops' own time  18.8 us (12%)
  between operations  17.3 us (11%)
  other arithmetic  10.3 us (6%)
  matrix products  2.43 us (2%)
    psum x1, blocking collectives, per_device(): summed = lax.psum((partial_terms[0],), ('grp', 'slab'))  42.7 us
    unnamed x1, blocking collectives  41.1 us
    another operation x1, loops' own time, entering(): return lax.fori_loop(0, count - 1, step, total)  18.8 us
    dynamic_slice x31, local copies, waits for them, and re-layouts, step(): longer = join(total, pieces[position])  18.3 us
    select_n x1, other arithmetic, per_device(): jnp.where(own_mask[None, None], own_basis, jnp.zeros((), jnp.bfloat16))  7.39 us
    unnamed x10, local copies, waits for them, and re-layouts  7.03 us
  transfers between devices with their start and end apart: 1, of which 0 were waited for; matrix products, arithmetic and copies ran while one was open for 11% of the time, Pallas kernels for 0%

commit v1 on v0

--- a/solution.py
+++ b/solution.py
@@ -4,6 +4,7 @@
 from jax.sharding import PartitionSpec as P
 
 PLANE = 512
+spread_slabs_up = lambda patch: jax.lax.psum(jax.lax.psum(patch, "slab"), "grp")
 
 
 def entering(value, axis, join, neutral):
@@ -48,7 +49,7 @@
         stacked, stacked, (((1,), (1,)), ((), ())), preferred_element_type=jnp.float32
     )
     partial_terms = (raw_gram,)
-    summed = lax.psum((partial_terms[0],), ("grp", "slab"))
+    summed = spread_slabs_up((partial_terms[0],))
     scales = jnp.concatenate([singular_values, jnp.ones((snap_count,), jnp.float32)])
     gram_matrix = summed[0] * scales[:, None] * scales[None, :] / (3.0 * live_cells)
     mixing = orthonormalize(gram_matrix[:, :rank_count], rank_count)

time: 161 us -> 202 us (1.25)
  blocking collectives: 83.8 us -> 124 us
    psum x1 -> x3, blocking collectives: 42.7 us -> 85.9 us  [the longest x1 42 us: per_device(): lax.psum(jnp.sum(thickness).astype(jnp.float32) * PLANE, ('grp', 'slab'))]
    unnamed x1, blocking collectives: 41.1 us -> 37.9 us
  transfers between devices with their start and end apart: 1 -> 1, of which waited for: 0 -> 0; matrix products, arithmetic and copies ran while one was open for 11% -> 9% of each run, Pallas kernels for 0% -> 0%
where the time goes in v1:
time: 202 us; the launch traced here: 200 us
  blocking collectives  124 us (61%)
  local copies, waits for them, and re-layouts  27.7 us (14%)
  loops' own time  18.8 us (9%)
  between operations  17.3 us (9%)
  other arithmetic  10.3 us (5%)
  matrix products  2.45 us (1%)
    psum x1, blocking collectives, per_device(): lax.psum(jnp.sum(thickness).astype(jnp.float32) * PLANE, ('grp', 'slab'))  42 us
    unnamed x1, blocking collectives  37.9 us
    psum x1, blocking collectives, jax.lax.psum(patch, 'slab')  27.2 us
    another operation x1, loops' own time, entering(): return lax.fori_loop(0, count - 1, step, total)  18.8 us
    dynamic_slice x31, local copies, waits for them, and re-layouts, step(): longer = join(total, pieces[position])  18.3 us
    psum x1, blocking collectives, jax.lax.psum(jax.lax.psum(patch, 'slab'), 'grp')  16.8 us
    select_n x1, other arithmetic, per_device(): jnp.where(own_mask[None, None], own_basis, jnp.zeros((), jnp.bfloat16))  7.39 us
    unnamed x10, local copies, waits for them, and re-layouts  6.82 us
  transfers between devices with their start and end apart: 1, of which 0 were waited for; matrix products, arithmetic and copies ran while one was open for 9% of the time, Pallas kernels for 0%

profile of v1, /device:TPU:0, one launch (start us, length us, event | category | flops | bytes accessed | tf_op | source)
XLA Modules:
  0.0 200.5 jit_solution(3278990580056632643)
XLA Ops:
  7.9 42.0 %psum.23 = f32[]{:T(128)} all-reduce(f32[]{:T(128)S(6)} %mul.67), channel_id=1, replica_groups=mesh['grp'=4,'slab'=8] {'grp','slab'}, use_global_device_ids=true, to_apply=%region_2.3 | all-reduce | flops 1 | bytes 8 | tf_op jit(solution)/shard_map/psum | solution.py:43
  49.9 2.2 %fusion.7 = bf16[16,3,2048]{2,1,0:T(4,128)(2,1)S(1)} fusion(pred[2048]{0:T(1024)(128)(4,1)S(1)} %fusion.11, f32[16,3,1,2048]{3,2,1,0:T(1,128)} %param.6), kind=kLoop, calls=%fused_computation.15 | loop fusion | flops 196608 | bytes 591872 | tf_op jit(solution)/shard_map/jit(_where)/select_n | solution.py:40
  52.3 7.4 %fusion = bf16[64,3,2048]{2,1,0:T(4,128)(2,1)S(1)} fusion(pred[2048]{0:T(1024)(128)(4,1)S(1)} %fusion.11, bf16[64,3,4,2048]{3,2,1,0:T(4,128)(2,1)} %param.7, s32[]{:T(128)S(6)} %select_n.42), kind=kLoop, calls=%fused_computation.3 | loop fusion | flops 393216 | bytes 1574916 | tf_op jit(solution)/shard_map/jit(_where)/select_n | solution.py:46
  59.6 0.6 copy.29
  60.8 27.2 %psum.21 = f32[80,80]{1,0:T(8,128)S(1)} all-reduce(f32[80,80]{1,0:T(8,128)S(1)} %fusion.15), channel_id=1, replica_groups=mesh['grp'=4,'slab'=8] {'slab'}, use_global_device_ids=true, to_apply=%region_0.1 | all-reduce | flops 6400 | bytes 51200 | tf_op jit(solution)/shard_map/psum | solution.py:7
  87.9 16.8 %psum.22 = f32[80,80]{1,0:T(8,128)S(1)} all-reduce(f32[80,80]{1,0:T(8,128)S(1)} %psum.21), channel_id=1, replica_groups=mesh['grp'=4,'slab'=8] {'grp'}, use_global_device_ids=true, to_apply=%region_1.2 | all-reduce | flops 6400 | bytes 51200 | tf_op jit(solution)/shard_map/psum | solution.py:7
  105.5 0.6 multiply_reduce_fusion
  108.9 1.2 reshape.69
  110.1 1.5 copy.21
  111.6 37.9 %all-reduce.1 = s32[32]{0:T(128)S(1)} all-reduce(s32[32]{0:T(128)S(1)} %bitcast_dynamic-update-slice_fusion), channel_id=2, replica_groups=mesh['grp'=4,'slab'=8] {'grp','slab'}, use_global_device_ids=true, to_apply=%add.1 | all-reduce | flops 32 | bytes 256
  149.5 37.0 %while.13 = (s32[]{:T(128)}, s32[1,1]{1,0:T(1,128)}, s32[]{:T(128)}, s32[32,1,1]{0,2,1:T(1,128)S(1)}, s32[]{:T(128)}) while((s32[]{:T(128)}, s32[1,1]{1,0:T(1,128)}, s32[]{:T(128)}, s32[32,1,1]{0,2,1:T(1,128)S(1)}, s32[]{:T(128)}) %tuple.42), condition=%wide.region_5.6_spmd, body=%wide.region_4.5_spmd.sunk | while | flops 5 | bytes 115 | solution.py:19
  150.7 0.6 constant_dynamic-slice_fusion.2
  151.9 0.6 constant_dynamic-slice_fusion.2
  155.4 0.6 constant_dynamic-slice_fusion.2
  156.6 0.6 constant_dynamic-slice_fusion.2
  157.8 0.6 constant_dynamic-slice_fusion.2
  159.0 0.6 constant_dynamic-slice_fusion.2
  162.6 0.6 constant_dynamic-slice_fusion.2
  163.8 0.6 constant_dynamic-slice_fusion.2
  165.0 0.6 constant_dynamic-slice_fusion.2
  166.2 0.6 constant_dynamic-slice_fusion.2
  167.4 0.6 constant_dynamic-slice_fusion.2
  171.0 0.6 constant_dynamic-slice_fusion.2
  186.5 6.0 %copy.23 = bf16[64,3,4,2048]{3,2,1,0:T(4,128)(2,1)} copy(bf16[64,3,4,2048]{3,0,1,2:T(8,128)(2,1)} %all-gather.3.cloned.1.call-done) | data formatting | bytes 6291456
  (44 shorter events, 14.1 us)
Async XLA Ops:
  7.2 179.4 %all-gather.3.cloned.1.call-start = ((), (), s32[]{:S(2)}) async-start(), calls=%async_computation | async-start | bytes 3932160 | tf_op jit(solution)/shard_map/all_gather | solution.py:58
  60.3 45.0 %copy-start.1 = (f32[64]{0:T(128)S(1)}, f32[64]{0:T(128)}, u32[]{:S(2)}) copy-start(f32[64]{0:T(128)} %param.8) | copy-start | bytes 772
  105.5 4.6 %copy-start = (f32[80,80]{1,0:T(8,128)}, f32[80,80]{1,0:T(8,128)S(1)}, u32[]{:S(2)}) copy-start(f32[80,80]{1,0:T(8,128)S(1)} %multiply_divide_fusion) | copy-start | bytes 76804
Sparse Core Ops, SparseCore 0:
  111.6 41.0 all-gather.2
